TPU v7x, 32 devices: a whole 2x2x4 slice. The times are simulated.
32 devices in a mesh: dp: 4 (over y, core), seq: 8 (over z, x).
Axes of the slice: x: 2, y: 2, z: 4, core: 2. Of those that a mesh axis runs over, the one named last changes fastest.
Arguments:
- queries: bfloat16 [32, 2048, 512], P('dp', 'seq'), may hold values from -6 to 6
- enc_keys: bfloat16 [32, 2048, 512], P('dp', 'seq'), may hold values from -6 to 6
- enc_values: bfloat16 [32, 2048, 512], P('dp', 'seq'), may hold values from -6 to 6
- dec_ids: int32 [32, 2048], P('dp', 'seq'), may hold values from 0 to 15, never falling along the last dimension, each value on 1 to 512 neighbouring positions
- enc_ids: int32 [32, 2048], P('dp', 'seq'), may hold values from 0 to 15, never falling along the last dimension, each value on 1 to 512 neighbouring positions
Outputs:
- context: bfloat16 [32, 2048, 512], P('dp', 'seq')
Inputs may be any that keep to these rules, and one draw needn't show every extreme that they name: `dec_ids`: along each row the numbers never fall; every number from 0 to 15 occurs in every row; a document holds 1 to 512 positions of a row, and some document holds exactly 512. `enc_ids`: along each row the numbers never fall; every number from 0 to 15 occurs in every row; a document holds 1 to 512 positions of a row, and some document holds exactly 512.
All inputs are finite; a program needn't handle non-finite values.
Results may differ from a plain program's by a relative error of at most 0.0047.
Values may be sent and summed in bfloat16 or wider, within the bound.
No kernel may reach another device: no remote copies, remote signals or barrier semaphores. Data moves between devices by JAX's collectives and lax.ppermute only.
A program may use at most 128 MiB of HBM per device.

v0:
```python
import jax
import jax.numpy as jnp
from jax import lax
from jax.sharding import PartitionSpec as P

HEAD_DIM = 64
masked_score = -1e30


def shortened(value):

    def short(part):
        return part.astype(jnp.bfloat16) if part.dtype == jnp.float32 else part

    return jax.tree.map(short, value)


def attend_dense(query_row, key_row, value_row, dec_row, enc_row, head_count):
    length = query_row.shape[0]
    query_heads = query_row.reshape(length, head_count, HEAD_DIM)
    key_heads = key_row.reshape(length, head_count, HEAD_DIM)
    value_heads = value_row.reshape(length, head_count, HEAD_DIM)
    query_span = min(512, length)
    pieces = []
    for offset in range(0, length, query_span):
        scores = jnp.einsum(
            "qhd,khd->hqk",
            query_heads[offset : offset + query_span],
            key_heads,
            preferred_element_type=jnp.float32,
        )
        allowed = (dec_row[offset : offset + query_span][:, None] == enc_row[None, :])[None]
        scores = jnp.where(allowed, scores, masked_score)
        row_peak = jnp.max(scores, axis=2, keepdims=True)
        expos = jnp.where(allowed, jnp.exp(scores - row_peak), 0.0)
        row_total = jnp.sum(expos, axis=2, keepdims=True)
        weights = (expos / row_total).astype(jnp.bfloat16)
        summed = jnp.einsum(
            "hqk,khd->qhd", weights, value_heads, preferred_element_type=jnp.float32
        )
        pieces.append(summed.reshape(query_span, head_count * HEAD_DIM).astype(jnp.bfloat16))
    return jnp.concatenate(pieces, axis=0)


def local(queries, enc_keys, enc_values, dec_ids, enc_ids):
    group = lax.axis_size("seq")
    dec_spread = jnp.broadcast_to(
        dec_ids.astype(jnp.bfloat16)[:, :, None], (dec_ids.shape[0], dec_ids.shape[1], group)
    )
    enc_spread = jnp.broadcast_to(
        enc_ids.astype(jnp.bfloat16)[:, :, None], (enc_ids.shape[0], enc_ids.shape[1], group)
    )
    members = (
        lax.all_to_all(queries, "seq", split_axis=2, concat_axis=1, tiled=True),
        lax.all_to_all(enc_keys, "seq", split_axis=2, concat_axis=1, tiled=True),
        lax.all_to_all(enc_values, "seq", split_axis=2, concat_axis=1, tiled=True),
        lax.all_to_all(dec_spread, "seq", split_axis=2, concat_axis=1, tiled=True),
        lax.all_to_all(enc_spread, "seq", split_axis=2, concat_axis=1, tiled=True),
    )
    dec_rows = members[3][:, :, 0].astype(jnp.int32)
    enc_rows = members[4][:, :, 0].astype(jnp.int32)
    query_rows = members[0]
    key_rows = members[1]
    value_rows = members[2]
    head_count = query_rows.shape[2] // HEAD_DIM

    def one_row(members):
        return attend_dense(members[0], members[1], members[2], members[3], members[4], head_count)

    attended = lax.map(one_row, (query_rows, key_rows, value_rows, dec_rows, enc_rows))
    return lax.all_to_all(
        shortened(attended), "seq", split_axis=1, concat_axis=2, tiled=True
    ).astype(attended.dtype)


def solution(mesh):
    in_specs = (
        P("dp", "seq", None),
        P("dp", "seq", None),
        P("dp", "seq", None),
        P("dp", "seq"),
        P("dp", "seq"),
    )
    out_specs = P("dp", "seq", None)
    return jax.shard_map(local, mesh=mesh, in_specs=in_specs, out_specs=out_specs, check_vma=False)
```

profile of v0, /device:TPU:0, one launch (start us, length us, event | category | flops | bytes accessed | tf_op | source)
XLA Modules:
  0.0 412.9 jit_solution(16733577638339409978)
XLA Ops:
  1.3 7.3 %all-to-all-start.1 = ((bf16[8,256,8]{1,0,2:T(8,128)(2,1)}), bf16[8,256,8]{1,0,2:T(8,128)(2,1)S(1)}, u32[]{:S(2)}, u32[]{:S(2)}) async-start(bf16[8,256,8]{1,0,2:T(8,128)(2,1)} %broadcast_in_dim.23), calls=%async_computation.1 | async-start | bytes 65536 | tf_op jit(solution)/shard_map/all_to_all | solution.py:57
  9.3 6.0 %all-to-all-done.1 = bf16[8,256,8]{1,0,2:T(8,128)(2,1)S(1)} async-done(((bf16[8,256,8]{1,0,2:T(8,128)(2,1)}), bf16[8,256,8]{1,0,2:T(8,128)(2,1)S(1)}, u32[]{:S(2)}, u32[]{:S(2)}) %all-to-all-start.1) | async-done | bytes 32800 | tf_op jit(solution)/shard_map/all_to_all | solution.py:57
  15.9 3.3 all-to-all-start.2
  19.2 4.5 %copy.25 = bf16[8,256,512]{1,0,2:T(8,128)(2,1)} copy(bf16[8,256,512]{2,1,0:T(8,128)(2,1)} %param.9) | data formatting | bytes 4194304 | tf_op args[2]
  23.7 2.1 all-to-all-done.2
  25.9 3.8 all-to-all-start
  29.7 4.5 %copy.28 = bf16[8,256,512]{1,0,2:T(8,128)(2,1)} copy(bf16[8,256,512]{2,1,0:T(8,128)(2,1)} %param.7) | data formatting | bytes 4194304 | tf_op args[0]
  34.2 42.1 %all-to-all-done = bf16[8,256,512]{1,0,2:T(8,128)(2,1)S(1)} async-done(((bf16[8,256,512]{1,0,2:T(8,128)(2,1)}), bf16[8,256,512]{1,0,2:T(8,128)(2,1)S(1)}, u32[]{:S(2)}, u32[]{:S(2)}) %all-to-all-start) | async-done | bytes 2097184 | tf_op jit(solution)/shard_map/all_to_all | solution.py:56
  76.3 4.4 %all-to-all-start.3 = ((bf16[8,256,512]{1,0,2:T(8,128)(2,1)}), bf16[8,256,512]{1,0,2:T(8,128)(2,1)}, u32[]{:S(2)}, u32[]{:S(2)}) async-start(bf16[8,256,512]{1,0,2:T(8,128)(2,1)} %copy.28), calls=%async_computation.3 | async-start | bytes 4194304 | tf_op jit(solution)/shard_map/all_to_all | solution.py:54
  80.7 4.5 %copy.31 = bf16[8,256,512]{1,0,2:T(8,128)(2,1)} copy(bf16[8,256,512]{2,1,0:T(8,128)(2,1)} %param.8) | data formatting | bytes 4194304 | tf_op args[1]
  85.2 43.1 %all-to-all-done.3 = bf16[8,256,512]{1,0,2:T(8,128)(2,1)} async-done(((bf16[8,256,512]{1,0,2:T(8,128)(2,1)}), bf16[8,256,512]{1,0,2:T(8,128)(2,1)}, u32[]{:S(2)}, u32[]{:S(2)}) %all-to-all-start.3) | async-done | bytes 2097184 | tf_op jit(solution)/shard_map/all_to_all | solution.py:54
  128.3 4.4 %all-to-all-start.4 = ((bf16[8,256,512]{1,0,2:T(8,128)(2,1)}), bf16[8,256,512]{1,0,2:T(8,128)(2,1)}, u32[]{:S(2)}, u32[]{:S(2)}) async-start(bf16[8,256,512]{1,0,2:T(8,128)(2,1)} %copy.31), calls=%async_computation.4 | async-start | bytes 4194304 | tf_op jit(solution)/shard_map/all_to_all | solution.py:55
  132.7 3.5 copy.42
  136.3 5.0 %copy.44 = bf16[8,8,256,64]{3,2,1,0:T(8,128)(2,1)} copy(bf16[8,8,256,64]{2,0,3,1:T(8,128)(2,1)} %bitcast.36) | data formatting | bytes 4194304 | tf_op jit(solution)/shard_map/while | solution.py:70
  141.3 39.2 %all-to-all-done.4 = bf16[8,256,512]{1,0,2:T(8,128)(2,1)} async-done(((bf16[8,256,512]{1,0,2:T(8,128)(2,1)}), bf16[8,256,512]{1,0,2:T(8,128)(2,1)}, u32[]{:S(2)}, u32[]{:S(2)}) %all-to-all-start.4) | async-done | bytes 2097184 | tf_op jit(solution)/shard_map/all_to_all | solution.py:55
  180.5 5.0 %copy.46 = bf16[8,8,256,64]{3,2,1,0:T(8,128)(2,1)} copy(bf16[8,8,256,64]{2,0,3,1:T(8,128)(2,1)} %bitcast.40) | data formatting | bytes 4194304 | tf_op jit(solution)/shard_map/while | solution.py:70
  185.5 150.7 %while.10 = (s32[]{:T(128)}, bf16[8,2048,64]{1,2,0:T(8,128)(2,1)S(1)}, bf16[8,2048,64]{2,1,0:T(8,128)(2,1)}, s32[8,2048]{1,0:T(8,128)S(1)}, s32[8,2048]{1,0:T(8,...) while((s32[]{:T(128)}, ...), condition=%wide.region_9.10_spmd, body=%wide.region_0.9_spmd.sunk | while | flops 1133637632 | bytes 72773864 | solution.py:70
  185.6 2.0 fusion.83
  189.4 1.8 fusion.84
  191.2 3.9 fusion.85
  196.5 3.4 fusion.86
  204.4 2.0 fusion.83
  210.1 3.9 fusion.85
  215.4 3.4 fusion.86
  223.3 2.0 fusion.83
  228.9 3.9 fusion.85
  234.2 3.4 fusion.86
  242.1 2.0 fusion.83
  247.7 3.9 fusion.85
  253.0 3.4 fusion.86
  260.9 2.0 fusion.83
  266.6 3.9 fusion.85
  271.9 3.4 fusion.86
  279.8 2.0 fusion.83
  285.4 3.9 fusion.85
  290.7 3.4 fusion.86
  298.6 2.0 fusion.83
  304.2 3.9 fusion.85
  309.6 3.4 fusion.86
  317.4 2.0 fusion.83
  323.1 3.9 fusion.85
  328.4 3.4 fusion.86
  336.2 4.3 %copy.37 = bf16[8,2048,64]{2,0,1:T(8,128)(2,1)} copy(bf16[8,2048,64]{1,2,0:T(8,128)(2,1)S(1)} %get-tuple-element.42) | data formatting | bytes 4194304 | tf_op jit(solution)/shard_map/while | solution.py:70
  340.5 6.4 %reshape.166 = bf16[8,2,65536]{2,1,0:T(2,128)(2,1)S(1)} reshape(bf16[2048,8,64]{2,1,0:T(8,128)(2,1)} %bitcast.147) | data formatting | bytes 4194304
  346.8 51.8 %all_to_all.90 = bf16[8,2,65536]{2,1,0:T(2,128)(2,1)} all-to-all(bf16[8,2,65536]{2,1,0:T(2,128)(2,1)S(1)} %reshape.166), channel_id=1, replica_groups=mesh['dp'=4,'seq'=8] {'seq'}, dimensions={0} | all-to-all | bytes 4194304 | tf_op jit(solution)/shard_map/all_to_all | solution.py:71
  398.7 7.4 %reshape.167 = bf16[2048,8,64]{2,1,0:T(8,128)(2,1)} reshape(bf16[8,2,65536]{2,1,0:T(2,128)(2,1)} %all_to_all.90) | data formatting | bytes 4194304
  406.1 4.5 %copy.39 = bf16[8,256,8,64]{1,3,2,0:T(8,128)(2,1)S(1)} copy(bf16[8,256,8,64]{3,0,1,2:T(8,128)(2,1)} %bitcast.148) | data formatting | bytes 4194304 | tf_op jit(solution)/shard_map/all_to_all | solution.py:71
  410.5 2.4 copy.40
  (96 shorter events, 77.0 us)
Async XLA Ops:
  1.3 14.0 %all-to-all-start.1 = ((bf16[8,256,8]{1,0,2:T(8,128)(2,1)}), bf16[8,256,8]{1,0,2:T(8,128)(2,1)S(1)}, u32[]{:S(2)}, u32[]{:S(2)}) async-start(bf16[8,256,8]{1,0,2:T(8,128)(2,1)} %broadcast_in_dim.23), calls=%async_computation.1 | async-start | bytes 65536 | tf_op jit(solution)/shard_map/all_to_all | solution.py:57
  15.9 10.0 %all-to-all-start.2 = ((bf16[8,256,8]{1,0,2:T(8,128)(2,1)}), bf16[8,256,8]{1,0,2:T(8,128)(2,1)S(1)}, u32[]{:S(2)}, u32[]{:S(2)}) async-start(bf16[8,256,8]{1,0,2:T(8,128)(2,1)} %broadcast_in_dim.24), calls=%async_computation.2 | async-start | bytes 65536 | tf_op jit(solution)/shard_map/all_to_all | solution.py:58
  25.9 50.4 %all-to-all-start = ((bf16[8,256,512]{1,0,2:T(8,128)(2,1)}), bf16[8,256,512]{1,0,2:T(8,128)(2,1)S(1)}, u32[]{:S(2)}, u32[]{:S(2)}) async-start(bf16[8,256,512]{1,0,2:T(8,128)(2,1)} %copy.25), calls=%async_computation | async-start | bytes 4194304 | tf_op jit(solution)/shard_map/all_to_all | solution.py:56
  76.3 52.0 %all-to-all-start.3 = ((bf16[8,256,512]{1,0,2:T(8,128)(2,1)}), bf16[8,256,512]{1,0,2:T(8,128)(2,1)}, u32[]{:S(2)}, u32[]{:S(2)}) async-start(bf16[8,256,512]{1,0,2:T(8,128)(2,1)} %copy.28), calls=%async_computation.3 | async-start | bytes 4194304 | tf_op jit(solution)/shard_map/all_to_all | solution.py:54
  128.3 52.2 %all-to-all-start.4 = ((bf16[8,256,512]{1,0,2:T(8,128)(2,1)}), bf16[8,256,512]{1,0,2:T(8,128)(2,1)}, u32[]{:S(2)}, u32[]{:S(2)}) async-start(bf16[8,256,512]{1,0,2:T(8,128)(2,1)} %copy.31), calls=%async_computation.4 | async-start | bytes 4194304 | tf_op jit(solution)/shard_map/all_to_all | solution.py:55
  141.3 44.2 %copy-start.1 = (bf16[8,2048,64]{1,2,0:T(8,128)(2,1)S(1)}, bf16[8,2048,64]{1,2,0:T(8,128)(2,1)}, u32[]{:S(2)}) copy-start(bf16[8,2048,64]{1,2,0:T(8,128)(2,1)} %custom-call) | copy-start | bytes 6291460
  191.2 3.9 copy-start
  210.0 3.9 copy-start
  228.9 3.9 copy-start
  247.7 3.9 copy-start
  266.6 3.9 copy-start
  285.4 3.9 copy-start
  304.2 3.9 copy-start
  323.1 3.9 copy-start
where the time goes:
time: 415 us; the launch traced here: 413 us
  waiting for transfers between devices  133 us (32%)
  matrix products  122 us (29%)
  local copies, waits for them, and re-layouts  54 us (13%)
  blocking collectives  51.8 us (12%)
  other arithmetic  29 us (7%)
  starting transfers between devices  23.1 us (6%)
    dot_general x32, matrix products, attend_dense(): jnp.einsum('qhd,khd->hqk', query_heads[offset:offset + query_span], key_h...  75.9 us
    all_to_all x1, blocking collectives, local(): lax.all_to_all(shortened(attended), 'seq', split_axis=1, concat_axis=2, t...  51.8 us
    dot_general x32, matrix products, attend_dense(): jnp.einsum('hqk,khd->qhd', weights, value_heads, preferred_element_type=j...  45.9 us
    all_to_all x1, waiting for transfers between devices, local(): lax.all_to_all(queries, 'seq', split_axis=2, concat_axis=1, tiled=True)  43.1 us
    all_to_all x1, waiting for transfers between devices, local(): lax.all_to_all(enc_values, 'seq', split_axis=2, concat_axis=1, tiled=True)  42.1 us
    all_to_all x1, waiting for transfers between devices, local(): lax.all_to_all(enc_keys, 'seq', split_axis=2, concat_axis=1, tiled=True)  39.2 us
    reduce_sum x8, other arithmetic, attend_dense(): row_total = jnp.sum(expos, axis=2, keepdims=True)  27.4 us
    unnamed x7, local copies, waits for them, and re-layouts  27.3 us
  transfers between devices with their start and end apart: 5, of which 5 were waited for; matrix products, arithmetic and copies ran while one was open for 6% of the time, Pallas kernels for 0%

commit v1 on v0

--- a/solution.py
+++ b/solution.py
@@ -68,8 +68,11 @@
         return attend_dense(members[0], members[1], members[2], members[3], members[4], head_count)
 
     attended = lax.map(one_row, (query_rows, key_rows, value_rows, dec_rows, enc_rows))
-    return lax.all_to_all(
-        shortened(attended), "seq", split_axis=1, concat_axis=2, tiled=True
+    return jnp.concatenate(
+        lax.all_to_all(
+            jnp.stack(jnp.split(shortened(attended), lax.axis_size("seq"), axis=1)), "seq", 0, 0
+        ),
+        axis=2,
     ).astype(attended.dtype)
 
 

time: 415 us -> 392 us (0.945)
  local copies, waits for them, and re-layouts: 54 us -> 31.9 us
    unnamed x7 -> x12, local copies, waits for them, and re-layouts: 27.3 us -> 13.8 us
    all_to_all x2 -> x1, local copies, waits for them, and re-layouts: 6.84 us -> 0.14 us  [local(): lax.all_to_all(jnp.stack(jnp.split(shortened(attended), lax.axis_size('se...]
    while x4 -> x3, local copies, waits for them, and re-layouts: 17.8 us -> 13.5 us  [local(): lax.map(one_row, (query_rows, key_rows, value_rows, dec_rows, enc_rows))]
where the time goes in v1:
time: 392 us; the launch traced here: 391 us
  waiting for transfers between devices  133 us (34%)
  matrix products  122 us (31%)
  blocking collectives  51.7 us (13%)
  local copies, waits for them, and re-layouts  31.9 us (8%)
  other arithmetic  29 us (7%)
  starting transfers between devices  23.1 us (6%)
    dot_general x32, matrix products, attend_dense(): jnp.einsum('qhd,khd->hqk', query_heads[offset:offset + query_span], key_h...  75.9 us
    all_to_all x1, blocking collectives, local(): lax.all_to_all(jnp.stack(jnp.split(shortened(attended), lax.axis_size('se...  51.7 us
    dot_general x32, matrix products, attend_dense(): jnp.einsum('hqk,khd->qhd', weights, value_heads, preferred_element_type=j...  45.9 us
    all_to_all x1, waiting for transfers between devices, local(): lax.all_to_all(queries, 'seq', split_axis=2, concat_axis=1, tiled=True)  43.1 us
    all_to_all x1, waiting for transfers between devices, local(): lax.all_to_all(enc_values, 'seq', split_axis=2, concat_axis=1, tiled=True)  42.1 us
    all_to_all x1, waiting for transfers between devices, local(): lax.all_to_all(enc_keys, 'seq', split_axis=2, concat_axis=1, tiled=True)  39.2 us
    reduce_sum x8, other arithmetic, attend_dense(): row_total = jnp.sum(expos, axis=2, keepdims=True)  27.4 us
    unnamed x12, local copies, waits for them, and re-layouts  13.8 us
  transfers between devices with their start and end apart: 5, of which 5 were waited for; matrix products, arithmetic and copies ran while one was open for 6% of the time, Pallas kernels for 0%

profile of v1, /device:TPU:0, one launch (start us, length us, event | category | flops | bytes accessed | tf_op | source)
XLA Modules:
  0.0 390.8 jit_solution(16948654742915008345)
XLA Ops:
  1.3 7.3 %all-to-all-start.1 = ((bf16[8,256,8]{1,0,2:T(8,128)(2,1)}), bf16[8,256,8]{1,0,2:T(8,128)(2,1)S(1)}, u32[]{:S(2)}, u32[]{:S(2)}) async-start(bf16[8,256,8]{1,0,2:T(8,128)(2,1)} %broadcast_in_dim.23), calls=%async_computation.1 | async-start | bytes 65536 | tf_op jit(solution)/shard_map/all_to_all | solution.py:57
  9.3 6.0 %all-to-all-done.1 = bf16[8,256,8]{1,0,2:T(8,128)(2,1)S(1)} async-done(((bf16[8,256,8]{1,0,2:T(8,128)(2,1)}), bf16[8,256,8]{1,0,2:T(8,128)(2,1)S(1)}, u32[]{:S(2)}, u32[]{:S(2)}) %all-to-all-start.1) | async-done | bytes 32800 | tf_op jit(solution)/shard_map/all_to_all | solution.py:57
  15.9 3.3 all-to-all-start.2
  19.2 4.5 %copy.24 = bf16[8,256,512]{1,0,2:T(8,128)(2,1)} copy(bf16[8,256,512]{2,1,0:T(8,128)(2,1)} %param.9) | data formatting | bytes 4194304 | tf_op args[2]
  23.7 2.1 all-to-all-done.2
  25.9 3.8 all-to-all-start
  29.7 4.5 %copy.27 = bf16[8,256,512]{1,0,2:T(8,128)(2,1)} copy(bf16[8,256,512]{2,1,0:T(8,128)(2,1)} %param.7) | data formatting | bytes 4194304 | tf_op args[0]
  34.2 42.1 %all-to-all-done = bf16[8,256,512]{1,0,2:T(8,128)(2,1)S(1)} async-done(((bf16[8,256,512]{1,0,2:T(8,128)(2,1)}), bf16[8,256,512]{1,0,2:T(8,128)(2,1)S(1)}, u32[]{:S(2)}, u32[]{:S(2)}) %all-to-all-start) | async-done | bytes 2097184 | tf_op jit(solution)/shard_map/all_to_all | solution.py:56
  76.3 4.4 %all-to-all-start.3 = ((bf16[8,256,512]{1,0,2:T(8,128)(2,1)}), bf16[8,256,512]{1,0,2:T(8,128)(2,1)}, u32[]{:S(2)}, u32[]{:S(2)}) async-start(bf16[8,256,512]{1,0,2:T(8,128)(2,1)} %copy.27), calls=%async_computation.3 | async-start | bytes 4194304 | tf_op jit(solution)/shard_map/all_to_all | solution.py:54
  80.7 4.5 %copy.30 = bf16[8,256,512]{1,0,2:T(8,128)(2,1)} copy(bf16[8,256,512]{2,1,0:T(8,128)(2,1)} %param.8) | data formatting | bytes 4194304 | tf_op args[1]
  85.2 43.1 %all-to-all-done.3 = bf16[8,256,512]{1,0,2:T(8,128)(2,1)} async-done(((bf16[8,256,512]{1,0,2:T(8,128)(2,1)}), bf16[8,256,512]{1,0,2:T(8,128)(2,1)}, u32[]{:S(2)}, u32[]{:S(2)}) %all-to-all-start.3) | async-done | bytes 2097184 | tf_op jit(solution)/shard_map/all_to_all | solution.py:54
  128.3 4.4 %all-to-all-start.4 = ((bf16[8,256,512]{1,0,2:T(8,128)(2,1)}), bf16[8,256,512]{1,0,2:T(8,128)(2,1)}, u32[]{:S(2)}, u32[]{:S(2)}) async-start(bf16[8,256,512]{1,0,2:T(8,128)(2,1)} %copy.30), calls=%async_computation.4 | async-start | bytes 4194304 | tf_op jit(solution)/shard_map/all_to_all | solution.py:55
  132.7 3.5 copy.39
  136.3 5.0 %copy.41 = bf16[8,8,256,64]{3,2,1,0:T(8,128)(2,1)} copy(bf16[8,8,256,64]{2,0,3,1:T(8,128)(2,1)} %bitcast.36) | data formatting | bytes 4194304 | tf_op jit(solution)/shard_map/while | solution.py:70
  141.3 39.2 %all-to-all-done.4 = bf16[8,256,512]{1,0,2:T(8,128)(2,1)} async-done(((bf16[8,256,512]{1,0,2:T(8,128)(2,1)}), bf16[8,256,512]{1,0,2:T(8,128)(2,1)}, u32[]{:S(2)}, u32[]{:S(2)}) %all-to-all-start.4) | async-done | bytes 2097184 | tf_op jit(solution)/shard_map/all_to_all | solution.py:55
  180.5 5.0 %copy.43 = bf16[8,8,256,64]{3,2,1,0:T(8,128)(2,1)} copy(bf16[8,8,256,64]{2,0,3,1:T(8,128)(2,1)} %bitcast.40) | data formatting | bytes 4194304 | tf_op jit(solution)/shard_map/while | solution.py:70
  185.5 150.7 %while.10 = (s32[]{:T(128)}, bf16[8,2048,64]{1,2,0:T(8,128)(2,1)S(1)}, bf16[8,2048,64]{2,1,0:T(8,128)(2,1)}, s32[8,2048]{1,0:T(8,128)S(1)}, s32[8,2048]{1,0:T(8,...) while((s32[]{:T(128)}, ...), condition=%wide.region_9.10_spmd, body=%wide.region_0.9_spmd.sunk | while | flops 1133637632 | bytes 72773864 | solution.py:70
  185.6 2.0 fusion.83
  189.4 1.8 fusion.84
  191.2 3.9 fusion.85
  196.5 3.4 fusion.86
  204.4 2.0 fusion.83
  208.2 1.8 fusion.84
  210.1 3.9 fusion.85
  215.4 3.4 fusion.86
  223.3 2.0 fusion.83
  227.0 1.8 fusion.84
  228.9 3.9 fusion.85
  234.2 3.4 fusion.86
  242.1 2.0 fusion.83
  245.9 1.8 fusion.84
  247.7 3.9 fusion.85
  253.0 3.4 fusion.86
  260.9 2.0 fusion.83
  264.7 1.8 fusion.84
  266.6 3.9 fusion.85
  271.9 3.4 fusion.86
  279.8 2.0 fusion.83
  285.4 3.9 fusion.85
  290.7 3.4 fusion.86
  298.6 2.0 fusion.83
  304.2 3.9 fusion.85
  309.6 3.4 fusion.86
  317.4 2.0 fusion.83
  323.1 3.9 fusion.85
  328.4 3.4 fusion.86
  336.5 51.7 %all_to_all.77 = bf16[8,8,256,64]{2,3,1,0:T(8,128)(2,1)S(1)} all-to-all(bf16[8,8,256,64]{2,3,1,0:T(8,128)(2,1)S(1)} %bitcast_dynamic-update-slice_fusion), channel_id=1, replica_groups=mesh['dp'=4,'seq'=8] {'seq'}, dimensions={0} | all-to-all | bytes 4194304 | tf_op jit(solution)/shard_map/all_to_all | solution.py:72
  388.4 2.4 copy.37
  (101 shorter events, 70.1 us)
Async XLA Ops:
  1.3 14.0 %all-to-all-start.1 = ((bf16[8,256,8]{1,0,2:T(8,128)(2,1)}), bf16[8,256,8]{1,0,2:T(8,128)(2,1)S(1)}, u32[]{:S(2)}, u32[]{:S(2)}) async-start(bf16[8,256,8]{1,0,2:T(8,128)(2,1)} %broadcast_in_dim.23), calls=%async_computation.1 | async-start | bytes 65536 | tf_op jit(solution)/shard_map/all_to_all | solution.py:57
  15.9 10.0 %all-to-all-start.2 = ((bf16[8,256,8]{1,0,2:T(8,128)(2,1)}), bf16[8,256,8]{1,0,2:T(8,128)(2,1)S(1)}, u32[]{:S(2)}, u32[]{:S(2)}) async-start(bf16[8,256,8]{1,0,2:T(8,128)(2,1)} %broadcast_in_dim.24), calls=%async_computation.2 | async-start | bytes 65536 | tf_op jit(solution)/shard_map/all_to_all | solution.py:58
  25.9 50.4 %all-to-all-start = ((bf16[8,256,512]{1,0,2:T(8,128)(2,1)}), bf16[8,256,512]{1,0,2:T(8,128)(2,1)S(1)}, u32[]{:S(2)}, u32[]{:S(2)}) async-start(bf16[8,256,512]{1,0,2:T(8,128)(2,1)} %copy.24), calls=%async_computation | async-start | bytes 4194304 | tf_op jit(solution)/shard_map/all_to_all | solution.py:56
  76.3 52.0 %all-to-all-start.3 = ((bf16[8,256,512]{1,0,2:T(8,128)(2,1)}), bf16[8,256,512]{1,0,2:T(8,128)(2,1)}, u32[]{:S(2)}, u32[]{:S(2)}) async-start(bf16[8,256,512]{1,0,2:T(8,128)(2,1)} %copy.27), calls=%async_computation.3 | async-start | bytes 4194304 | tf_op jit(solution)/shard_map/all_to_all | solution.py:54
  128.3 52.2 %all-to-all-start.4 = ((bf16[8,256,512]{1,0,2:T(8,128)(2,1)}), bf16[8,256,512]{1,0,2:T(8,128)(2,1)}, u32[]{:S(2)}, u32[]{:S(2)}) async-start(bf16[8,256,512]{1,0,2:T(8,128)(2,1)} %copy.30), calls=%async_computation.4 | async-start | bytes 4194304 | tf_op jit(solution)/shard_map/all_to_all | solution.py:55
  141.3 44.2 %copy-start.1 = (bf16[8,2048,64]{1,2,0:T(8,128)(2,1)S(1)}, bf16[8,2048,64]{1,2,0:T(8,128)(2,1)}, u32[]{:S(2)}) copy-start(bf16[8,2048,64]{1,2,0:T(8,128)(2,1)} %custom-call.1) | copy-start | bytes 6291460
  191.2 3.9 copy-start
  210.0 3.9 copy-start
  228.9 3.9 copy-start
  247.7 3.9 copy-start
  266.6 3.9 copy-start
  285.4 3.9 copy-start
  304.2 3.9 copy-start
  323.1 3.9 copy-start
